TPU v7x, 32 devices: a whole 2x2x4 slice. The times are simulated.
32 devices in a mesh: row: 4 (over y, core), col: 8 (over z, x).
Axes of the slice: x: 2, y: 2, z: 4, core: 2. Of those that a mesh axis runs over, the one named last changes fastest.
Arguments:
- amplitudes: float32 [2, 32, 1048576], P(None, 'row', 'col'), may hold values from -6 to 6
- qubit_order: int32 [11], replicated, may hold values from 0 to 10, each once
Outputs:
- correlators: float32 [8, 131072], P('col', 'row')
Inputs may be any that keep to these rules, and one draw needn't show every extreme that they name: `qubit_order`: a permutation of 0 to 10.
All inputs are finite; a program needn't handle non-finite values.
Results may differ from a plain program's by a relative error of at most 0.0003.
Values sent between devices are 32-bit elements; how exact they have to be, the bound alone decides.
No kernel may reach another device: no remote copies, remote signals or barrier semaphores. Data moves between devices by JAX's collectives and lax.ppermute only.
A program may use at most 64 MiB of HBM per device.

v0:
```python
import jax
import jax.numpy as jnp
from jax import lax
from jax.sharding import PartitionSpec as P

MEASURED_QUBITS = 20


def from_partner(x, axis, stride):
    return lax.ppermute(x, axis, [(i, i ^ 1 << stride) for i in range(lax.axis_size(axis))])


def source_index(qubit_order):
    count = qubit_order.shape[0]
    target = jnp.arange(2**count, dtype=jnp.int32)
    source = jnp.zeros_like(target)
    for bit_location in range(count):
        bit_value = jnp.bitwise_and(jnp.right_shift(target, bit_location), 1)
        source = source + jnp.left_shift(bit_value, qubit_order[bit_location])
    return source


def reorder_bits(values, qubit_order):
    perm_span = 2 ** qubit_order.shape[0]
    return jnp.take(values.reshape(-1, perm_span), source_index(qubit_order), axis=1).reshape(-1)


def hadamard_matrix(count):
    extent = 2**count
    row_ids = jnp.arange(extent, dtype=jnp.int32)[:, None]
    col_ids = jnp.arange(extent, dtype=jnp.int32)[None, :]
    common = jnp.bitwise_and(row_ids, col_ids)
    parity = jnp.zeros((extent, extent), jnp.int32)
    for bit_location in range(count):
        parity = parity + jnp.bitwise_and(jnp.right_shift(common, bit_location), 1)
    return (1 - 2 * jnp.bitwise_and(parity, 1)).astype(jnp.float32)


def transform_last(values):
    height, length = values.shape
    total_bits = length.bit_length() - 1
    offset = 0
    while offset < total_bits:
        group_bits = min(7, total_bits - offset)
        group_size = 2**group_bits
        matrix = hadamard_matrix(group_bits)
        blocks = values.reshape(height, length // (group_size * 2**offset), group_size, 2**offset)
        blocks = jnp.einsum("ij,rajb->raib", matrix, blocks, precision=lax.Precision.HIGHEST)
        values = blocks.reshape(height, length)
        offset = offset + group_bits
    return values


def column_butterfly_steps(values):
    for bit_location in range(lax.axis_size("col").bit_length() - 1):
        partner = from_partner(values, "col", bit_location)
        high_bit = jnp.bitwise_and(jnp.right_shift(lax.axis_index("col"), bit_location), 1)
        values = jnp.where(high_bit == 0, values + partner, partner - values)
    return values


def local(amplitudes, qubit_order):
    partial_value = jnp.sum(amplitudes * amplitudes, axis=(0, 1))
    probability_total = lax.psum(jnp.sum(partial_value), ("row", "col"))
    row_count = lax.axis_size("row")
    share = partial_value.shape[0] // row_count
    summed = lax.psum(partial_value, "row")
    walsh_coefficients = transform_last(summed.reshape(1, -1)).reshape(-1)
    locally_held = lax.dynamic_slice_in_dim(
        walsh_coefficients, lax.axis_index("row") * share, share
    )
    locally_held = reorder_bits(locally_held, qubit_order)
    locally_held = column_butterfly_steps(locally_held)
    normalized_result = locally_held * 2.0 ** (MEASURED_QUBITS / 2) / probability_total
    return normalized_result.reshape(1, -1)


def solution(mesh):
    in_specs = (P(None, "row", "col"), P())
    out_specs = P("col", "row")
    return jax.shard_map(local, mesh=mesh, in_specs=in_specs, out_specs=out_specs, check_vma=False)
```

profile of v0, /device:TPU:0, one launch (start us, length us, event | category | flops | bytes accessed | tf_op | source)
XLA Modules:
  0.0 121.8 jit_solution(10911104259614391344)
XLA Ops:
  6.5 0.0 copy-start
  6.5 0.0 all-reduce.2.cloned.1.call-start
  6.5 8.7 %multiply_reduce_fusion = (f32[]{:T(128)}, f32[131072]{0:T(1024)}) fusion(f32[2,8,131072]{2,1,0:T(8,128)} %param.2), kind=kLoop, calls=%fused_computation.1 | loop fusion | flops 6160383 | bytes 8912900 | tf_op jit(solution)/shard_map/reduce_sum | solution.py:64
  15.2 0.0 all-reduce.2.cloned.1.call-update
  15.2 0.0 copy-done
  15.2 0.7 fusion.42
  15.9 7.0 %compare_select_fusion = s32[2048,1]{0,1:T(1,128)S(1)} fusion(s32[]{:T(128)} %bitcast.10, s32[]{:T(128)} %bitcast.9, s32[]{:T(128)} %bitcast.8, s32[]{:T(128)} %bitcast.7, s32[]{:T(128)} %bitcast.6, s32[]{:T(128)} %bitcast.5, s32[]{:T(128)} %bitcast.4, s32[]{:T(128)} %bitcast.3, s32[]{:T(128)} %bitcast.2, s32[]{:T(128)} %bitcast.1, s32[]{:T(128)} %bitcast), kind=kLoop, calls=%fused_computation.17 | loop fusion | flops 94208 | bytes 8236 | tf_op jit(solution)/shard_map/jit(_take)/jit(_where)/select_n | solution.py:25
  22.9 6.9 %compare_and_fusion = pred[2048]{0:T(1024)(128)(4,1)S(1)} fusion(s32[]{:T(128)} %bitcast.10, s32[]{:T(128)} %bitcast.9, s32[]{:T(128)} %bitcast.8, s32[]{:T(128)} %bitcast.7, s32[]{:T(128)} %bitcast.6, s32[]{:T(128)} %bitcast.5, s32[]{:T(128)} %bitcast.4, s32[]{:T(128)} %bitcast.3, s32[]{:T(128)} %bitcast.2, s32[]{:T(128)} %bitcast.1, s32[]{:T(128)} %bitcast), kind=kLoop, calls=%fused_computation.19 | loop fusion | flops 100352 | bytes 2092 | tf_op jit(solution)/shard_map/jit(_take)/and | solution.py:25
  29.8 21.7 %all-reduce.2.cloned.1.call-done = f32[8,128,128]{2,1,0:T(8,128)} async-done(((f32[8,128,128]{2,1,0:T(8,128)}), f32[8,128,128]{2,1,0:T(8,128)}) %all-reduce.2.cloned.1.call-update) | async-done | bytes 524304 | tf_op jit(solution)/shard_map/psum | solution.py:67
  51.5 1.7 %fusion.3 = f32[8,128,128]{1,2,0:T(8,128)S(1)} fusion(f32[8,128,128]{2,1,0:T(8,128)} %all-reduce.2.cloned.1.call-done), kind=kOutput, calls=%fused_computation.12 | convolution fusion | flops 201736192 | bytes 1048576 | tf_op jit(solution)/shard_map/ij,rajb->raib/dot_general | solution.py:48
  53.2 0.6 convolution_bitcast_fusion.1
  53.8 0.2 copy.3
  54.0 0.9 convolution_bitcast_fusion
  54.9 0.1 copy.7
  55.1 0.3 copy.4
  55.4 5.5 %gather_fusion = f32[2048,16]{1,0:T(8,128)S(1)} fusion(f32[16,2048]{0,1:T(8,128)S(1)} %copy.4, s32[2048]{0:T(1024)S(1)} %broadcast_clamp_fusion), kind=kCustom, calls=%fused_computation | custom fusion | bytes 270336 | tf_op jit(solution)/shard_map/jit(_take)/gather | solution.py:25
  60.9 0.3 select_bitcast_fusion
  61.3 0.3 copy.5
  61.6 1.5 %collective-permute-start = (f32[32768]{0:T(1024)S(1)}, f32[32768]{0:T(1024)S(1)}, u32[]{:S(2)}, u32[]{:S(2)}) collective-permute-start(f32[32768]{0:T(1024)S(1)} %bitcast.43), channel_id=1, source_target_pairs={{0,1},{1,0},{2,3},{3,2},{4,5},{5,4},{6,7},{7,6},{8,9},{9,8},{10,11... | collective-permute-start | bytes 393224 | tf_op jit(solution)/shard_map/ppermute | solution.py:10
  63.1 3.5 %collective-permute-done = f32[32768]{0:T(1024)S(1)} collective-permute-done((f32[32768]{0:T(1024)S(1)}, f32[32768]{0:T(1024)S(1)}, u32[]{:S(2)}, u32[]{:S(2)}) %collective-permute-start) | collective-permute-done | bytes 131104 | tf_op jit(solution)/shard_map/ppermute | solution.py:10
  66.7 1.6 %collective-permute-start.1 = (f32[32768]{0:T(1024)S(1)}, f32[32768]{0:T(1024)S(1)}, u32[]{:S(2)}, u32[]{:S(2)}) collective-permute-start(f32[32768]{0:T(1024)S(1)} %subtract_select_fusion.1), channel_id=1, source_target_pairs={{0,2},{1,3},{2,0},{3,1},{4,6},{5,7},{6,4},{7,5},{8,10},{9,11},{10,... | collective-permute-start | bytes 393224 | tf_op jit(solution)/shard_map/ppermute | solution.py:10
  68.2 3.5 %collective-permute-done.1 = f32[32768]{0:T(1024)S(1)} collective-permute-done((f32[32768]{0:T(1024)S(1)}, f32[32768]{0:T(1024)S(1)}, u32[]{:S(2)}, u32[]{:S(2)}) %collective-permute-start.1) | collective-permute-done | bytes 131104 | tf_op jit(solution)/shard_map/ppermute | solution.py:10
  71.7 3.2 %collective-permute-start.2 = (f32[32768]{0:T(1024)S(1)}, f32[32768]{0:T(1024)S(1)}, u32[]{:S(2)}, u32[]{:S(2)}) collective-permute-start(f32[32768]{0:T(1024)S(1)} %subtract_select_fusion), channel_id=1, source_target_pairs={{0,4},{1,5},{2,6},{3,7},{4,0},{5,1},{6,2},{7,3},{8,12},{9,13},{10,... | collective-permute-start | bytes 393224 | tf_op jit(solution)/shard_map/ppermute | solution.py:10
  74.9 38.7 %psum.15 = f32[]{:T(128)} all-reduce(f32[]{:T(128)} %get-tuple-element.5), channel_id=1, replica_groups=mesh['row'=4,'col'=8] {'row','col'}, use_global_device_ids=true, to_apply=%region_3.0 | all-reduce | flops 1 | bytes 8 | tf_op jit(solution)/shard_map/psum | solution.py:64
  113.6 0.0 collective-permute-done.2
  113.6 1.4 %multiply_divide_fusion = f32[32768]{0:T(1024)} fusion(f32[32768]{0:T(1024)S(1)} %collective-permute-done.2, f32[32768]{0:T(1024)S(1)} %subtract_select_fusion, f32[]{:T(128)} %psum.15, pred[]{:T(512)S(6)} %eq.9), kind=kLoop, calls=%fused_computation.8 | loop fusion | flops 163840 | bytes 393221 | tf_op jit(solution)/shard_map/div | solution.py:74
  (6 shorter events, 0.1 us)
Async XLA Ops:
  6.5 8.7 %copy-start = (s32[11]{0:T(128)S(1)}, s32[11]{0:T(128)}, u32[]{:S(2)}) copy-start(s32[11]{0:T(128)} %param.3) | copy-start | bytes 136
  6.5 45.0 %all-reduce.2.cloned.1.call-start = ((), (), s32[]{:S(2)}) async-start(), calls=%async_computation | async-start | bytes 1048576 | tf_op jit(solution)/shard_map/psum | solution.py:67
  61.6 5.0 %collective-permute-start = (f32[32768]{0:T(1024)S(1)}, f32[32768]{0:T(1024)S(1)}, u32[]{:S(2)}, u32[]{:S(2)}) collective-permute-start(f32[32768]{0:T(1024)S(1)} %bitcast.43), channel_id=1, source_target_pairs={{0,1},{1,0},{2,3},{3,2},{4,5},{5,4},{6,7},{7,6},{8,9},{9,8},{10,11... | collective-permute-start | bytes 393224 | tf_op jit(solution)/shard_map/ppermute | solution.py:10
  66.7 5.0 %collective-permute-start.1 = (f32[32768]{0:T(1024)S(1)}, f32[32768]{0:T(1024)S(1)}, u32[]{:S(2)}, u32[]{:S(2)}) collective-permute-start(f32[32768]{0:T(1024)S(1)} %subtract_select_fusion.1), channel_id=1, source_target_pairs={{0,2},{1,3},{2,0},{3,1},{4,6},{5,7},{6,4},{7,5},{8,10},{9,11},{10,... | collective-permute-start | bytes 393224 | tf_op jit(solution)/shard_map/ppermute | solution.py:10
  71.7 41.9 %collective-permute-start.2 = (f32[32768]{0:T(1024)S(1)}, f32[32768]{0:T(1024)S(1)}, u32[]{:S(2)}, u32[]{:S(2)}) collective-permute-start(f32[32768]{0:T(1024)S(1)} %subtract_select_fusion), channel_id=1, source_target_pairs={{0,4},{1,5},{2,6},{3,7},{4,0},{5,1},{6,2},{7,3},{8,12},{9,13},{10,... | collective-permute-start | bytes 393224 | tf_op jit(solution)/shard_map/ppermute | solution.py:10
Sparse Core Ops, SparseCore 0:
  15.3 36.1 all-reduce.1
where the time goes:
time: 122 us
  blocking collectives  38.7 us (32%)
  waiting for transfers between devices  28.8 us (24%)
  other arithmetic  24.2 us (20%)
  between operations  13.5 us (11%)
  local copies, waits for them, and re-layouts  7.16 us (6%)
  starting transfers between devices  6.32 us (5%)
  matrix products  3.19 us (3%)
    psum x1, blocking collectives, local(): probability_total = lax.psum(jnp.sum(partial_value), ('row', 'col'))  38.7 us
    psum x1, waiting for transfers between devices, local(): summed = lax.psum(partial_value, 'row')  21.7 us
    reduce_sum x1, other arithmetic, local(): probability_total = lax.psum(jnp.sum(partial_value), ('row', 'col'))  8.65 us
    select_n x2, other arithmetic, reorder_bits(): jnp.take(values.reshape(-1, perm_span), source_index(qubit_order), axis=1)  7.29 us
    ppermute x3, waiting for transfers between devices, from_partner(): lax.ppermute(x, axis, [(i, i ^ 1 << stride) for i in range(lax.axis_size(...  6.99 us
    and x1, other arithmetic, reorder_bits(): jnp.take(values.reshape(-1, perm_span), source_index(qubit_order), axis=1)  6.87 us
    ppermute x3, starting transfers between devices, from_partner(): lax.ppermute(x, axis, [(i, i ^ 1 << stride) for i in range(lax.axis_size(...  6.31 us
    gather x1, local copies, waits for them, and re-layouts, reorder_bits(): jnp.take(values.reshape(-1, perm_span), source_index(qubit_order), axis=1)  5.47 us
  transfers between devices with their start and end apart: 4, of which 3 were waited for; matrix products, arithmetic and copies ran while one was open for 12% of the time, Pallas kernels for 0%

commit v1 on v0

v1 whole, which is shorter than its diff:
```python
import jax
import jax.numpy as jnp
from jax import lax
from jax.experimental import pallas as pl
from jax.experimental.pallas import tpu as pltpu
from jax.sharding import PartitionSpec as P

LANES = 128
SUB = 8
ROW_SIDE = 16
CHUNK = ROW_SIDE * ROW_SIDE * LANES


def log2(n):
    return n.bit_length() - 1


def parity_sign(common, bits):
    shift = 1
    while shift < bits:
        common = jnp.bitwise_xor(common, jnp.right_shift(common, shift))
        shift *= 2
    return (1 - 2 * jnp.bitwise_and(common, 1)).astype(jnp.float32)


def iota(shape, axis):
    return lax.broadcasted_iota(jnp.int32, shape, axis)


def bit_of(values, position):
    return jnp.bitwise_and(jnp.right_shift(values, position), 1)


def split(values):
    high = values.astype(jnp.bfloat16)
    low = (values - high.astype(jnp.float32)).astype(jnp.bfloat16)
    return jnp.concatenate([high, low], axis=1)


def transform_kernel(order, amps, out, mass, buf, xs, hrow, hlane, inverse, rows_moved, lanes_moved, sems):
    parts, groups, length = buf.shape[0], buf.shape[1] // SUB, buf.shape[2]
    chunks = length // CHUNK
    half = CHUNK // 2
    lane_bits, row_bits = log2(LANES), log2(ROW_SIDE)
    count = order.shape[0]

    def copies(c):
        return [
            pltpu.make_async_copy(
                amps.at[p, :, pl.ds(c * CHUNK + h * half, half)],
                buf.at[p, :, pl.ds(c * CHUNK + h * half, half)],
                sems.at[c, p, h],
            )
            for p in range(parts)
            for h in range(2)
        ]

    for c in range(min(2, chunks)):
        for copy in copies(c):
            copy.start()

    for j in range(count):
        inverse[order[j]] = j
    for p in range(count + 1):
        rows_moved[p] = lane_bits
        lanes_moved[p] = 0
    moved = jnp.int32(0)
    for p in range(lane_bits, count):
        rows_moved[moved] = p
        moved = moved + (inverse[p] < lane_bits).astype(jnp.int32)
    moved = jnp.int32(0)
    for p in range(lane_bits):
        lanes_moved[moved] = p
        moved = moved + (inverse[p] >= lane_bits).astype(jnp.int32)

    lane = iota((1, LANES), 1)
    zero = jnp.zeros((1, LANES), jnp.int32)
    lane_index, row_flip, lane_from_row = zero, zero, [jnp.int32(0)] * row_bits
    rank = jnp.int32(0)
    for p in range(lane_bits):
        crosses = inverse[p] >= lane_bits
        partner = rows_moved[rank]
        source = jnp.where(crosses, inverse[jnp.where(crosses, partner, 0)], inverse[p])
        lane_index = lane_index + jnp.left_shift(bit_of(lane, source), p)
        row_flip = row_flip + jnp.where(crosses, jnp.left_shift(bit_of(lane, p), partner - lane_bits), 0)
        for r in range(row_bits):
            lane_from_row[r] = lane_from_row[r] + jnp.where(
                jnp.logical_and(crosses, partner == lane_bits + r), jnp.int32(1 << p), jnp.int32(0)
            )
        rank = rank + crosses.astype(jnp.int32)

    out_row_flip, row_target = zero, []
    rank = jnp.int32(0)
    for p in range(lane_bits, count):
        crosses = inverse[p] < lane_bits
        out_row_flip = out_row_flip + jnp.where(
            crosses, jnp.left_shift(bit_of(lane, jnp.where(crosses, inverse[p], 0)), p - lane_bits), 0
        )
        partner = lanes_moved[rank]
        row_target.append(jnp.where(crosses, inverse[jnp.where(crosses, partner, 0)], inverse[p]) - lane_bits)
        rank = rank + crosses.astype(jnp.int32)

    side = ROW_SIDE * ROW_SIDE
    column = iota((1, side), 1)
    low = jnp.right_shift(column, row_bits)
    low_target = jnp.zeros((1, side), jnp.int32)
    for p in range(row_bits):
        low_target = low_target + jnp.left_shift(bit_of(low, p), row_target[p])
    source = jnp.left_shift(jnp.bitwise_and(column, ROW_SIDE - 1), row_bits) + low_target
    hrow[...] = parity_sign(jnp.bitwise_and(iota((side, side), 0), source), 2 * row_bits).astype(jnp.bfloat16)
    stacked = (2 * LANES, LANES)
    lane_sign = parity_sign(
        jnp.bitwise_and(jnp.bitwise_and(iota(stacked, 0), LANES - 1), iota(stacked, 1)), lane_bits
    )
    hlane[...] = lane_sign.astype(jnp.bfloat16)

    flips = [bit_of(row_flip, r) == 1 for r in range(row_bits)]
    out_flips = [bit_of(out_row_flip, r) == 1 for r in range(row_bits)]
    gathers = []
    for i in range(ROW_SIDE):
        moved = jnp.int32(0)
        for r in range(row_bits):
            if i >> r & 1:
                moved = moved + lane_from_row[r]
        gathers.append(jnp.broadcast_to(jnp.bitwise_xor(lane_index, moved), (ROW_SIDE, LANES)))

    sub = iota((SUB, LANES), 0)
    masks = [bit_of(sub, level) == 0 for level in range(log2(SUB))]

    def packed_row(base, i, upper):
        tiles = []
        for s in range(SUB):
            start = base + ((upper * SUB + s) * ROW_SIDE + i) * LANES
            total = None
            for p in range(parts):
                for g in range(groups):
                    v = buf[p, g * SUB : (g + 1) * SUB, pl.ds(start, LANES)]
                    total = v * v if total is None else total + v * v
            tiles.append(total)
        for level in range(log2(SUB)):
            merged = []
            for k in range(0, len(tiles), 2):
                a, b = tiles[k], tiles[k + 1]
                kept = jnp.where(masks[level], a, b)
                other = jnp.where(masks[level], b, a)
                merged.append(kept + pltpu.roll(other, SUB - (1 << level), 0))
            tiles = merged
        return tiles[0]

    def flip_rows(rows, which):
        for r in range(row_bits):
            rows = [jnp.where(which[r], rows[i ^ 1 << r], rows[i]) for i in range(ROW_SIDE)]
        return rows

    def one_chunk(c, total):
        for copy in copies(c):
            copy.wait()

        @pl.when(c + 2 < chunks)
        def _():
            for copy in copies(c + 2):
                copy.start()

        base = pl.multiple_of(c * CHUNK, CHUNK)
        for i in range(ROW_SIDE):
            for upper in range(ROW_SIDE // SUB):
                packed = packed_row(base, i, upper)
                total = total + packed
                xs[i, upper * SUB : (upper + 1) * SUB, :] = packed
        rows = flip_rows([xs[i] for i in range(ROW_SIDE)], flips)
        rows = [jnp.take_along_axis(rows[i], gathers[i], axis=1) for i in range(ROW_SIDE)]
        rows = flip_rows(rows, out_flips)
        x = split(jnp.concatenate(rows, axis=0))
        y = jnp.dot(hrow[...], x, preferred_element_type=jnp.float32)
        y = split(y[:, :LANES] + y[:, LANES:])
        z = jnp.dot(y, hlane[...], preferred_element_type=jnp.float32)
        out[pl.ds(pl.multiple_of(c * side, side), side), :] = z
        return total

    mass[...] = lax.fori_loop(0, chunks, one_chunk, jnp.zeros((SUB, LANES), jnp.float32))

    stride = 1
    while stride < chunks:
        for c in range(chunks):
            if c & stride == 0:
                a_rows, b_rows = pl.ds(c * side, side), pl.ds((c + stride) * side, side)
                a, b = out[a_rows, :], out[b_rows, :]
                out[a_rows, :] = a + b
                out[b_rows, :] = a - b
        stride *= 2


def transform_local(amplitudes, qubit_order):
    parts, unmeasured, length = amplitudes.shape
    chunks = length // CHUNK
    side = ROW_SIDE * ROW_SIDE
    count = qubit_order.shape[0]
    return pl.pallas_call(
        transform_kernel,
        out_shape=(
            jax.ShapeDtypeStruct((chunks * side, LANES), jnp.float32),
            jax.ShapeDtypeStruct((SUB, LANES), jnp.float32),
        ),
        in_specs=[pl.BlockSpec(memory_space=pltpu.SMEM), pl.BlockSpec(memory_space=pl.ANY)],
        out_specs=(pl.BlockSpec(memory_space=pltpu.VMEM), pl.BlockSpec(memory_space=pltpu.VMEM)),
        scratch_shapes=[
            pltpu.VMEM((parts, unmeasured, length), jnp.float32),
            pltpu.VMEM((ROW_SIDE, ROW_SIDE, LANES), jnp.float32),
            pltpu.VMEM((side, side), jnp.bfloat16),
            pltpu.VMEM((2 * LANES, LANES), jnp.bfloat16),
            pltpu.SMEM((count,), jnp.int32),
            pltpu.SMEM((count + 1,), jnp.int32),
            pltpu.SMEM((count + 1,), jnp.int32),
            pltpu.SemaphoreType.DMA((chunks, parts, 2)),
        ],
        name="transform_local",
    )(qubit_order, amplitudes)


def exchange(message, axis, position):
    size = lax.axis_size(axis)
    return lax.ppermute(message, axis, [(i, i ^ 1 << position) for i in range(size)])


def local(amplitudes, qubit_order, measured_qubits):
    values, mass = transform_local(amplitudes, qubit_order)
    blocks = lax.axis_size("row")
    share = values.shape[0] // blocks
    for position in range(log2(blocks)):
        pairs = values.reshape(-1, 2, share, LANES)
        high = bit_of(lax.axis_index("row"), position) == 1
        kept = jnp.where(high, pairs[:, 1], pairs[:, 0]).reshape(-1, LANES)
        sent = jnp.where(high, pairs[:, 0], pairs[:, 1]).reshape(-1, LANES)
        received = exchange(jnp.concatenate([sent, mass]), "row", position)
        joined = jnp.concatenate([kept, mass]) + received
        values, mass = joined[:-SUB], joined[-SUB:]
    joined = jnp.concatenate([values, mass])
    plain = iota((joined.shape[0], 1), 0) >= share
    for position in range(log2(lax.axis_size("col"))):
        received = exchange(joined, "col", position)
        low = bit_of(lax.axis_index("col"), position) == 0
        joined = received + jnp.where(jnp.logical_or(plain, low), joined, -joined)
    total = jnp.sum(joined[-SUB:])
    return (joined[:-SUB] * 2.0 ** (measured_qubits / 2) / total).reshape(1, -1)


def solution(mesh):
    def program(amplitudes, qubit_order):
        measured_qubits = log2(amplitudes.shape[2])
        return jax.shard_map(
            lambda a, q: local(a, q, measured_qubits),
            mesh=mesh,
            in_specs=(P(None, "row", "col"), P()),
            out_specs=P("col", "row"),
            check_vma=False,
        )(amplitudes, qubit_order)

    return program
```

time: 122 us -> 37.8 us (0.31)
  blocking collectives: 38.7 us -> 0 us
  other arithmetic: 24.2 us -> 4.7 us
  between operations: 13.5 us -> 0.08 us
  waiting for transfers between devices: 28.8 us -> 16.1 us
  local copies, waits for them, and re-layouts: 7.16 us -> 0.02 us
  Pallas kernels: 0 us -> 6.44 us
  starting transfers between devices: 6.32 us -> 10.3 us
  matrix products: 3.19 us -> 0 us
    psum x1 -> x0, blocking collectives: 38.7 us -> none  [local(): probability_total = lax.psum(jnp.sum(partial_value), ('row', 'col'))]
    psum x1 -> x0, waiting for transfers between devices: 21.7 us -> none  [local(): summed = lax.psum(partial_value, 'row')]
    ppermute x3 -> x5, waiting for transfers between devices: 6.99 us -> 16.1 us  [exchange(): lax.ppermute(message, axis, [(i, i ^ 1 << position) for i in range(size)])]
    reduce_sum x1, other arithmetic: 8.65 us -> 0.59 us  [local(): total = jnp.sum(joined[-SUB:])]
    and x1 -> x0, other arithmetic: 6.87 us -> none  [reorder_bits(): jnp.take(values.reshape(-1, perm_span), source_index(qubit_order), axis=1)]
    pallas_call x0 -> x1, Pallas kernels: none -> 6.44 us  [transform_local(): pl.pallas_call(transform_kernel, out_shape=(jax.ShapeDtypeStruct((chunks...]
    select_n x4 -> x2, other arithmetic: 7.32 us -> 1.1 us  [local(): kept = jnp.where(high, pairs[:, 1], pairs[:, 0]).reshape(-1, LANES)]
    gather x1 -> x0, local copies, waits for them, and re-layouts: 5.47 us -> none  [reorder_bits(): jnp.take(values.reshape(-1, perm_span), source_index(qubit_order), axis=1)]
  transfers between devices with their start and end apart: 4 -> 5, of which waited for: 3 -> 5; matrix products, arithmetic and copies ran while one was open for 12% -> 0% of each run, Pallas kernels for 0% -> 0%
where the time goes in v1:
time: 37.8 us; the launch traced here: 37.6 us
  waiting for transfers between devices  16.1 us (43%)
  starting transfers between devices  10.3 us (27%)
  Pallas kernels  6.44 us (17%)
  other arithmetic  4.7 us (12%)
    ppermute x5, waiting for transfers between devices, exchange(): lax.ppermute(message, axis, [(i, i ^ 1 << position) for i in range(size)])  16.1 us
    ppermute x5, starting transfers between devices, exchange(): lax.ppermute(message, axis, [(i, i ^ 1 << position) for i in range(size)])  10.3 us
    pallas_call x1, Pallas kernels, transform_local(): pl.pallas_call(transform_kernel, out_shape=(jax.ShapeDtypeStruct((chunks...  6.44 us
    div x1, other arithmetic, local(): return (joined[:-SUB] * 2.0 ** (measured_qubits / 2) / total).reshape(1, -1)  1.23 us
    select_n x2, other arithmetic, local(): kept = jnp.where(high, pairs[:, 1], pairs[:, 0]).reshape(-1, LANES)  1.1 us
  transfers between devices with their start and end apart: 5, of which 5 were waited for; matrix products, arithmetic and copies ran while one was open for 0% of the time, Pallas kernels for 0%

profile of v1, /device:TPU:0, one launch (start us, length us, event | category | flops | bytes accessed | tf_op | source)
XLA Modules:
  0.0 37.6 jit_solution(1533755544001624730)
XLA Ops:
  0.0 6.4 %transform_local.1 = (f32[1024,128]{1,0:T(8,128)}, f32[8,128]{1,0:T(8,128)}) custom-call(s32[11]{0:T(128)} %order.1, f32[2,8,131072]{2,1,0:T(8,128)} %amps.1), custom_call_target="tpu_custom_call" | custom-call | tf_op jit(solution)/shard_map/transform_local/pallas_call | solution.py:198
  6.5 1.1 %slice_select_fusion.1 = (f32[2,1,256,128]{3,2,1,0:T(8,128)S(1)}, f32[2,1,256,128]{3,2,1,0:T(8,128)S(1)}) fusion(f32[2,2,256,128]{3,2,1,0:T(8,128)} %bitcast.12, pred[]{:T(512)S(6)} %eq.16), kind=kLoop, calls=%fused_computation.4 | loop fusion | flops 131072 | bytes 1048577 | tf_op jit(solution)/shard_map/jit(_where)/select_n | solution.py:232
  7.5 0.7 %pad_maximum_fusion = f32[520,128]{1,0:T(8,128)S(1)} fusion(f32[8,128]{1,0:T(8,128)} %get-tuple-element.8, f32[512,128]{1,0:T(8,128)S(1)} %bitcast.11), kind=kLoop, calls=%fused_computation | loop fusion | flops 66560 | bytes 532480 | tf_op jit(solution)/shard_map/concatenate | solution.py:234
  8.2 0.6 %collective-permute-start = (f32[520,128]{1,0:T(8,128)S(1)}, f32[520,128]{1,0:T(8,128)S(1)}, u32[]{:S(2)}, u32[]{:S(2)}) collective-permute-start(f32[520,128]{1,0:T(8,128)S(1)} %pad_maximum_fusion), channel_id=1, source_target_pairs={{0,8},{8,0},{16,24},{24,16},{1,9},{9,1},{17,25},{25,17},{2,10},{10... | collective-permute-start | bytes 798728 | tf_op jit(solution)/shard_map/ppermute | solution.py:222
  8.8 1.2 %collective-permute-done = f32[520,128]{1,0:T(8,128)S(1)} collective-permute-done((f32[520,128]{1,0:T(8,128)S(1)}, f32[520,128]{1,0:T(8,128)S(1)}, u32[]{:S(2)}, u32[]{:S(2)}) %collective-permute-start) | collective-permute-done | bytes 266272 | tf_op jit(solution)/shard_map/ppermute | solution.py:222
  10.0 0.7 %fusion = f32[520,128]{1,0:T(8,128)S(1)} fusion(f32[520,128]{1,0:T(8,128)S(1)} %collective-permute-done, f32[8,128]{1,0:T(8,128)} %get-tuple-element.8, f32[512,128]{1,0:T(8,128)S(1)} %bitcast.10), kind=kLoop, calls=%fused_computation.2 | loop fusion | flops 133120 | bytes 798720 | tf_op jit(solution)/shard_map/add | solution.py:235
  10.8 2.9 %collective-permute-start.1 = (f32[264,128]{1,0:T(8,128)S(1)}, f32[264,128]{1,0:T(8,128)S(1)}, u32[]{:S(2)}, u32[]{:S(2)}) collective-permute-start(f32[264,128]{1,0:T(8,128)S(1)} %pad_maximum_fusion.2), channel_id=1, source_target_pairs={{0,16},{8,24},{16,0},{24,8},{1,17},{9,25},{17,1},{25,9},{2,18},{10... | collective-permute-start | bytes 405512 | tf_op jit(solution)/shard_map/ppermute | solution.py:222
  13.7 3.9 %collective-permute-done.1 = f32[264,128]{1,0:T(8,128)S(1)} collective-permute-done((f32[264,128]{1,0:T(8,128)S(1)}, f32[264,128]{1,0:T(8,128)S(1)}, u32[]{:S(2)}, u32[]{:S(2)}) %collective-permute-start.1) | collective-permute-done | bytes 135200 | tf_op jit(solution)/shard_map/ppermute | solution.py:222
  17.6 1.8 %collective-permute-start.2 = (f32[264,128]{1,0:T(8,128)S(1)}, f32[264,128]{1,0:T(8,128)S(1)}, u32[]{:S(2)}, u32[]{:S(2)}) collective-permute-start(f32[264,128]{1,0:T(8,128)S(1)} %fusion.1), channel_id=1, source_target_pairs={{0,1},{1,0},{2,3},{3,2},{4,5},{5,4},{6,7},{7,6},{8,9},{9,8},{10,11... | collective-permute-start | bytes 405512 | tf_op jit(solution)/shard_map/ppermute | solution.py:222
  19.4 3.3 %collective-permute-done.2 = f32[264,128]{1,0:T(8,128)S(1)} collective-permute-done((f32[264,128]{1,0:T(8,128)S(1)}, f32[264,128]{1,0:T(8,128)S(1)}, u32[]{:S(2)}, u32[]{:S(2)}) %collective-permute-start.2) | collective-permute-done | bytes 135200 | tf_op jit(solution)/shard_map/ppermute | solution.py:222
  22.7 0.1 fusion.2
  22.8 1.8 %collective-permute-start.3 = (f32[264,128]{1,0:T(8,128)S(1)}, f32[264,128]{1,0:T(8,128)S(1)}, u32[]{:S(2)}, u32[]{:S(2)}) collective-permute-start(f32[264,128]{1,0:T(8,128)S(1)} %fusion.2), channel_id=1, source_target_pairs={{0,2},{1,3},{2,0},{3,1},{4,6},{5,7},{6,4},{7,5},{8,10},{9,11},{10,... | collective-permute-start | bytes 405512 | tf_op jit(solution)/shard_map/ppermute | solution.py:222
  24.7 3.2 %collective-permute-done.3 = f32[264,128]{1,0:T(8,128)S(1)} collective-permute-done((f32[264,128]{1,0:T(8,128)S(1)}, f32[264,128]{1,0:T(8,128)S(1)}, u32[]{:S(2)}, u32[]{:S(2)}) %collective-permute-start.3) | collective-permute-done | bytes 135200 | tf_op jit(solution)/shard_map/ppermute | solution.py:222
  27.9 0.1 fusion.3
  28.0 3.2 %collective-permute-start.4 = (f32[264,128]{1,0:T(8,128)S(1)}, f32[264,128]{1,0:T(8,128)S(1)}, u32[]{:S(2)}, u32[]{:S(2)}) collective-permute-start(f32[264,128]{1,0:T(8,128)S(1)} %fusion.3), channel_id=1, source_target_pairs={{0,4},{1,5},{2,6},{3,7},{4,0},{5,1},{6,2},{7,3},{8,12},{9,13},{10,... | collective-permute-start | bytes 405512 | tf_op jit(solution)/shard_map/ppermute | solution.py:222
  31.2 4.4 %collective-permute-done.4 = f32[264,128]{1,0:T(8,128)S(1)} collective-permute-done((f32[264,128]{1,0:T(8,128)S(1)}, f32[264,128]{1,0:T(8,128)S(1)}, u32[]{:S(2)}, u32[]{:S(2)}) %collective-permute-start.4) | collective-permute-done | bytes 135200 | tf_op jit(solution)/shard_map/ppermute | solution.py:222
  35.7 0.1 fusion.4
  35.8 0.6 %slice_reduce_fusion = f32[]{:T(128)} fusion(f32[264,128]{1,0:T(8,128)S(1)} %fusion.4), kind=kLoop, calls=%fused_computation.18 | loop fusion | flops 1023 | bytes 4100 | tf_op jit(solution)/shard_map/reduce_sum | solution.py:243
  36.4 1.2 %fusion.5 = f32[256,128]{1,0:T(8,128)} fusion(f32[264,128]{1,0:T(8,128)S(1)} %fusion.4, f32[]{:T(128)} %slice_reduce_fusion), kind=kLoop, calls=%fused_computation.15 | loop fusion | flops 65536 | bytes 262148 | tf_op jit(solution)/shard_map/div | solution.py:244
  (8 shorter events, 0.1 us)
Async XLA Ops:
  8.2 1.7 %collective-permute-start = (f32[520,128]{1,0:T(8,128)S(1)}, f32[520,128]{1,0:T(8,128)S(1)}, u32[]{:S(2)}, u32[]{:S(2)}) collective-permute-start(f32[520,128]{1,0:T(8,128)S(1)} %pad_maximum_fusion), channel_id=1, source_target_pairs={{0,8},{8,0},{16,24},{24,16},{1,9},{9,1},{17,25},{25,17},{2,10},{10... | collective-permute-start | bytes 798728 | tf_op jit(solution)/shard_map/ppermute | solution.py:222
  10.8 6.8 %collective-permute-start.1 = (f32[264,128]{1,0:T(8,128)S(1)}, f32[264,128]{1,0:T(8,128)S(1)}, u32[]{:S(2)}, u32[]{:S(2)}) collective-permute-start(f32[264,128]{1,0:T(8,128)S(1)} %pad_maximum_fusion.2), channel_id=1, source_target_pairs={{0,16},{8,24},{16,0},{24,8},{1,17},{9,25},{17,1},{25,9},{2,18},{10... | collective-permute-start | bytes 405512 | tf_op jit(solution)/shard_map/ppermute | solution.py:222
  17.6 5.1 %collective-permute-start.2 = (f32[264,128]{1,0:T(8,128)S(1)}, f32[264,128]{1,0:T(8,128)S(1)}, u32[]{:S(2)}, u32[]{:S(2)}) collective-permute-start(f32[264,128]{1,0:T(8,128)S(1)} %fusion.1), channel_id=1, source_target_pairs={{0,1},{1,0},{2,3},{3,2},{4,5},{5,4},{6,7},{7,6},{8,9},{9,8},{10,11... | collective-permute-start | bytes 405512 | tf_op jit(solution)/shard_map/ppermute | solution.py:222
  22.8 5.1 %collective-permute-start.3 = (f32[264,128]{1,0:T(8,128)S(1)}, f32[264,128]{1,0:T(8,128)S(1)}, u32[]{:S(2)}, u32[]{:S(2)}) collective-permute-start(f32[264,128]{1,0:T(8,128)S(1)} %fusion.2), channel_id=1, source_target_pairs={{0,2},{1,3},{2,0},{3,1},{4,6},{5,7},{6,4},{7,5},{8,10},{9,11},{10,... | collective-permute-start | bytes 405512 | tf_op jit(solution)/shard_map/ppermute | solution.py:222
  28.0 7.6 %collective-permute-start.4 = (f32[264,128]{1,0:T(8,128)S(1)}, f32[264,128]{1,0:T(8,128)S(1)}, u32[]{:S(2)}, u32[]{:S(2)}) collective-permute-start(f32[264,128]{1,0:T(8,128)S(1)} %fusion.3), channel_id=1, source_target_pairs={{0,4},{1,5},{2,6},{3,7},{4,0},{5,1},{6,2},{7,3},{8,12},{9,13},{10,... | collective-permute-start | bytes 405512 | tf_op jit(solution)/shard_map/ppermute | solution.py:222

commit v2 on v1

--- a/solution.py
+++ b/solution.py
@@ -1,3 +1,5 @@
+import functools
+
 import jax
 import jax.numpy as jnp
 from jax import lax
@@ -37,7 +39,7 @@
     return jnp.concatenate([high, low], axis=1)
 
 
-def transform_kernel(order, amps, out, mass, buf, xs, hrow, hlane, inverse, rows_moved, lanes_moved, sems):
+def transform_kernel(row_axis, order, amps, sent, kept, buf, out, xs, hrow, hlane, inverse, rows_moved, lanes_moved, sems):
     parts, groups, length = buf.shape[0], buf.shape[1] // SUB, buf.shape[2]
     chunks = length // CHUNK
     half = CHUNK // 2
@@ -177,7 +179,8 @@
         out[pl.ds(pl.multiple_of(c * side, side), side), :] = z
         return total
 
-    mass[...] = lax.fori_loop(0, chunks, one_chunk, jnp.zeros((SUB, LANES), jnp.float32))
+    total = lax.fori_loop(0, chunks, one_chunk, jnp.zeros((SUB, LANES), jnp.float32))
+    total = jnp.broadcast_to(jnp.sum(total, keepdims=True), (SUB, LANES))
 
     stride = 1
     while stride < chunks:
@@ -189,22 +192,30 @@
                 out[b_rows, :] = a - b
         stride *= 2
 
-
-def transform_local(amplitudes, qubit_order):
+    blocks = lax.axis_size(row_axis)
+    share = out.shape[0] // blocks
+    own_bit = bit_of(lax.axis_index(row_axis), 0)
+    for ref, bit in ((sent, 1 - own_bit), (kept, own_bit)):
+        for pair in range(blocks // 2):
+            start = pl.multiple_of((2 * pair + bit) * share, share)
+            ref[pair * share : (pair + 1) * share, :] = out[pl.ds(start, share), :]
+        ref[blocks // 2 * share :, :] = total
+
+
+def transform_local(amplitudes, qubit_order, row_axis):
     parts, unmeasured, length = amplitudes.shape
     chunks = length // CHUNK
     side = ROW_SIDE * ROW_SIDE
     count = qubit_order.shape[0]
+    message = pltpu.VMEM((chunks * side // 2 + SUB, LANES), jnp.float32)
     return pl.pallas_call(
-        transform_kernel,
-        out_shape=(
-            jax.ShapeDtypeStruct((chunks * side, LANES), jnp.float32),
-            jax.ShapeDtypeStruct((SUB, LANES), jnp.float32),
-        ),
+        functools.partial(transform_kernel, row_axis),
+        out_shape=(message, message),
         in_specs=[pl.BlockSpec(memory_space=pltpu.SMEM), pl.BlockSpec(memory_space=pl.ANY)],
         out_specs=(pl.BlockSpec(memory_space=pltpu.VMEM), pl.BlockSpec(memory_space=pltpu.VMEM)),
         scratch_shapes=[
             pltpu.VMEM((parts, unmeasured, length), jnp.float32),
+            pltpu.VMEM((chunks * side, LANES), jnp.float32),
             pltpu.VMEM((ROW_SIDE, ROW_SIDE, LANES), jnp.float32),
             pltpu.VMEM((side, side), jnp.bfloat16),
             pltpu.VMEM((2 * LANES, LANES), jnp.bfloat16),
@@ -223,25 +234,25 @@
 
 
 def local(amplitudes, qubit_order, measured_qubits):
-    values, mass = transform_local(amplitudes, qubit_order)
-    blocks = lax.axis_size("row")
-    share = values.shape[0] // blocks
-    for position in range(log2(blocks)):
-        pairs = values.reshape(-1, 2, share, LANES)
+    sent, kept = transform_local(amplitudes, qubit_order, "row")
+    joined = kept + exchange(sent, "row", 0)
+    row_bits = log2(lax.axis_size("row"))
+    share = (joined.shape[0] - SUB) >> row_bits - 1
+    for position in range(1, row_bits):
+        pairs = joined[:-SUB].reshape(-1, 2, share, LANES)
+        mass = joined[-SUB:]
         high = bit_of(lax.axis_index("row"), position) == 1
         kept = jnp.where(high, pairs[:, 1], pairs[:, 0]).reshape(-1, LANES)
         sent = jnp.where(high, pairs[:, 0], pairs[:, 1]).reshape(-1, LANES)
-        received = exchange(jnp.concatenate([sent, mass]), "row", position)
-        joined = jnp.concatenate([kept, mass]) + received
-        values, mass = joined[:-SUB], joined[-SUB:]
-    joined = jnp.concatenate([values, mass])
-    plain = iota((joined.shape[0], 1), 0) >= share
+        joined = jnp.concatenate([kept, mass]) + exchange(jnp.concatenate([sent, mass]), "row", position)
+    values, mass = joined[:-SUB], joined[-SUB:]
     for position in range(log2(lax.axis_size("col"))):
-        received = exchange(joined, "col", position)
-        low = bit_of(lax.axis_index("col"), position) == 0
-        joined = received + jnp.where(jnp.logical_or(plain, low), joined, -joined)
-    total = jnp.sum(joined[-SUB:])
-    return (joined[:-SUB] * 2.0 ** (measured_qubits / 2) / total).reshape(1, -1)
+        received = exchange(jnp.concatenate([values, mass]), "col", position)
+        sign = 1.0 - 2.0 * bit_of(lax.axis_index("col"), position).astype(jnp.float32)
+        values = received[:-SUB] + values * sign
+        mass = received[-SUB:] + mass
+    total = mass[:1]
+    return (values * 2.0 ** (measured_qubits / 2) / total).reshape(1, -1)
 
 
 def solution(mesh):

time: 37.8 us -> 33.2 us (0.88)
  other arithmetic: 4.7 us -> 0.83 us
  Pallas kernels: 6.44 us -> 5.7 us
    select_n x2 -> x1, other arithmetic: 1.1 us -> 0.02 us  [local(): kept = jnp.where(high, pairs[:, 1], pairs[:, 0]).reshape(-1, LANES)]
    add x5 -> x7, other arithmetic: 1.04 us -> 0.1 us  [the longest x1 0.04 us: local(): joined = kept + exchange(sent, 'row', 0)]
    pallas_call x1, Pallas kernels: 6.44 us -> 5.7 us  [transform_local(): pl.pallas_call(functools.partial(transform_kernel, row_axis), out_shape=(...]
    concatenate x2 -> x3, other arithmetic: 0.72 us -> 0.03 us  [the longest x2 0.02 us: local(): received = exchange(jnp.concatenate([values, mass]), 'col', position)]
    reduce_sum x1 -> x0, other arithmetic: 0.59 us -> none  [local(): total = jnp.sum(joined[-SUB:])]
    div x1, other arithmetic: 1.23 us -> 0.68 us  [local(): return (values * 2.0 ** (measured_qubits / 2) / total).reshape(1, -1)]
where the time goes in v2:
time: 33.2 us; the launch traced here: 33.1 us
  waiting for transfers between devices  16.1 us (48%)
  starting transfers between devices  10.4 us (31%)
  Pallas kernels  5.7 us (17%)
  other arithmetic  0.83 us (2%)
    ppermute x5, waiting for transfers between devices, exchange(): lax.ppermute(message, axis, [(i, i ^ 1 << position) for i in range(size)])  16.1 us
    ppermute x5, starting transfers between devices, exchange(): lax.ppermute(message, axis, [(i, i ^ 1 << position) for i in range(size)])  10.4 us
    pallas_call x1, Pallas kernels, transform_local(): pl.pallas_call(functools.partial(transform_kernel, row_axis), out_shape=(...  5.7 us
    div x1, other arithmetic, local(): return (values * 2.0 ** (measured_qubits / 2) / total).reshape(1, -1)  0.68 us
  transfers between devices with their start and end apart: 5, of which 5 were waited for; matrix products, arithmetic and copies ran while one was open for 0% of the time, Pallas kernels for 0%

profile of v2, /device:TPU:0, one launch (start us, length us, event | category | flops | bytes accessed | tf_op | source)
XLA Modules:
  0.0 33.1 jit_solution(13332674661020351534)
XLA Ops:
  0.0 5.7 %transform_local.1 = (f32[520,128]{1,0:T(8,128)S(1)}, f32[520,128]{1,0:T(8,128)S(1)}) custom-call(s32[11]{0:T(128)} %order.1, f32[2,8,131072]{2,1,0:T(8,128)} %amps.1), custom_call_target="tpu_custom_call" | custom-call | tf_op jit(solution)/shard_map/transform_local/pallas_call | solution.py:211
  5.7 0.6 %collective-permute-start = (f32[520,128]{1,0:T(8,128)S(1)}, f32[520,128]{1,0:T(8,128)S(1)}, u32[]{:S(2)}, u32[]{:S(2)}) collective-permute-start(f32[520,128]{1,0:T(8,128)S(1)} %get-tuple-element.8), channel_id=1, source_target_pairs={{0,8},{8,0},{16,24},{24,16},{1,9},{9,1},{17,25},{25,17},{2,10},{10... | collective-permute-start | bytes 798728 | tf_op jit(solution)/shard_map/ppermute | solution.py:233
  6.3 1.2 %collective-permute-done = f32[520,128]{1,0:T(8,128)S(1)} collective-permute-done((f32[520,128]{1,0:T(8,128)S(1)}, f32[520,128]{1,0:T(8,128)S(1)}, u32[]{:S(2)}, u32[]{:S(2)}) %collective-permute-start) | collective-permute-done | bytes 266272 | tf_op jit(solution)/shard_map/ppermute | solution.py:233
  7.6 2.9 %collective-permute-start.1 = (f32[264,128]{1,0:T(8,128)S(1)}, f32[264,128]{1,0:T(8,128)S(1)}, u32[]{:S(2)}, u32[]{:S(2)}) collective-permute-start(f32[264,128]{1,0:T(8,128)S(1)} %pad_maximum_fusion), channel_id=1, source_target_pairs={{0,16},{8,24},{16,0},{24,8},{1,17},{9,25},{17,1},{25,9},{2,18},{10... | collective-permute-start | bytes 405512 | tf_op jit(solution)/shard_map/ppermute | solution.py:233
  10.5 3.9 %collective-permute-done.1 = f32[264,128]{1,0:T(8,128)S(1)} collective-permute-done((f32[264,128]{1,0:T(8,128)S(1)}, f32[264,128]{1,0:T(8,128)S(1)}, u32[]{:S(2)}, u32[]{:S(2)}) %collective-permute-start.1) | collective-permute-done | bytes 135200 | tf_op jit(solution)/shard_map/ppermute | solution.py:233
  14.4 1.8 %collective-permute-start.2 = (f32[264,128]{1,0:T(8,128)S(1)}, f32[264,128]{1,0:T(8,128)S(1)}, u32[]{:S(2)}, u32[]{:S(2)}) collective-permute-start(f32[264,128]{1,0:T(8,128)S(1)} %fusion), channel_id=1, source_target_pairs={{0,1},{1,0},{2,3},{3,2},{4,5},{5,4},{6,7},{7,6},{8,9},{9,8},{10,11... | collective-permute-start | bytes 405512 | tf_op jit(solution)/shard_map/ppermute | solution.py:233
  16.2 3.3 %collective-permute-done.2 = f32[264,128]{1,0:T(8,128)S(1)} collective-permute-done((f32[264,128]{1,0:T(8,128)S(1)}, f32[264,128]{1,0:T(8,128)S(1)}, u32[]{:S(2)}, u32[]{:S(2)}) %collective-permute-start.2) | collective-permute-done | bytes 135200 | tf_op jit(solution)/shard_map/ppermute | solution.py:233
  19.6 1.8 %collective-permute-start.3 = (f32[264,128]{1,0:T(8,128)S(1)}, f32[264,128]{1,0:T(8,128)S(1)}, u32[]{:S(2)}, u32[]{:S(2)}) collective-permute-start(f32[264,128]{1,0:T(8,128)S(1)} %pad_maximum_fusion.2), channel_id=1, source_target_pairs={{0,2},{1,3},{2,0},{3,1},{4,6},{5,7},{6,4},{7,5},{8,10},{9,11},{10,... | collective-permute-start | bytes 405512 | tf_op jit(solution)/shard_map/ppermute | solution.py:233
  21.4 3.3 %collective-permute-done.3 = f32[264,128]{1,0:T(8,128)S(1)} collective-permute-done((f32[264,128]{1,0:T(8,128)S(1)}, f32[264,128]{1,0:T(8,128)S(1)}, u32[]{:S(2)}, u32[]{:S(2)}) %collective-permute-start.3) | collective-permute-done | bytes 135200 | tf_op jit(solution)/shard_map/ppermute | solution.py:233
  24.7 3.3 %collective-permute-start.4 = (f32[264,128]{1,0:T(8,128)S(1)}, f32[264,128]{1,0:T(8,128)S(1)}, u32[]{:S(2)}, u32[]{:S(2)}) collective-permute-start(f32[264,128]{1,0:T(8,128)S(1)} %pad_maximum_fusion.3), channel_id=1, source_target_pairs={{0,4},{1,5},{2,6},{3,7},{4,0},{5,1},{6,2},{7,3},{8,12},{9,13},{10,... | collective-permute-start | bytes 405512 | tf_op jit(solution)/shard_map/ppermute | solution.py:233
  28.0 4.4 %collective-permute-done.4 = f32[264,128]{1,0:T(8,128)S(1)} collective-permute-done((f32[264,128]{1,0:T(8,128)S(1)}, f32[264,128]{1,0:T(8,128)S(1)}, u32[]{:S(2)}, u32[]{:S(2)}) %collective-permute-start.4) | collective-permute-done | bytes 135200 | tf_op jit(solution)/shard_map/ppermute | solution.py:233
  32.4 0.7 %fusion.2 = f32[256,128]{1,0:T(8,128)} fusion(f32[264,128]{1,0:T(8,128)S(1)} %collective-permute-done.4, f32[256,128]{1,0:T(8,128)S(1)} %slice_add_fusion.1, f32[128]{0:T(128)S(1)} %slice_bitcast_fusion, f32[]{:T(128)S(6)} %sub.11), kind=kLoop, calls=%fused_computation.7 | loop fusion | flops 131072 | bytes 393732 | tf_op jit(solution)/shard_map/div | solution.py:255
  (14 shorter events, 0.2 us)
Async XLA Ops:
  5.7 1.7 %collective-permute-start = (f32[520,128]{1,0:T(8,128)S(1)}, f32[520,128]{1,0:T(8,128)S(1)}, u32[]{:S(2)}, u32[]{:S(2)}) collective-permute-start(f32[520,128]{1,0:T(8,128)S(1)} %get-tuple-element.8), channel_id=1, source_target_pairs={{0,8},{8,0},{16,24},{24,16},{1,9},{9,1},{17,25},{25,17},{2,10},{10... | collective-permute-start | bytes 798728 | tf_op jit(solution)/shard_map/ppermute | solution.py:233
  7.6 6.8 %collective-permute-start.1 = (f32[264,128]{1,0:T(8,128)S(1)}, f32[264,128]{1,0:T(8,128)S(1)}, u32[]{:S(2)}, u32[]{:S(2)}) collective-permute-start(f32[264,128]{1,0:T(8,128)S(1)} %pad_maximum_fusion), channel_id=1, source_target_pairs={{0,16},{8,24},{16,0},{24,8},{1,17},{9,25},{17,1},{25,9},{2,18},{10... | collective-permute-start | bytes 405512 | tf_op jit(solution)/shard_map/ppermute | solution.py:233
  14.4 5.1 %collective-permute-start.2 = (f32[264,128]{1,0:T(8,128)S(1)}, f32[264,128]{1,0:T(8,128)S(1)}, u32[]{:S(2)}, u32[]{:S(2)}) collective-permute-start(f32[264,128]{1,0:T(8,128)S(1)} %fusion), channel_id=1, source_target_pairs={{0,1},{1,0},{2,3},{3,2},{4,5},{5,4},{6,7},{7,6},{8,9},{9,8},{10,11... | collective-permute-start | bytes 405512 | tf_op jit(solution)/shard_map/ppermute | solution.py:233
  19.6 5.1 %collective-permute-start.3 = (f32[264,128]{1,0:T(8,128)S(1)}, f32[264,128]{1,0:T(8,128)S(1)}, u32[]{:S(2)}, u32[]{:S(2)}) collective-permute-start(f32[264,128]{1,0:T(8,128)S(1)} %pad_maximum_fusion.2), channel_id=1, source_target_pairs={{0,2},{1,3},{2,0},{3,1},{4,6},{5,7},{6,4},{7,5},{8,10},{9,11},{10,... | collective-permute-start | bytes 405512 | tf_op jit(solution)/shard_map/ppermute | solution.py:233
  24.7 7.7 %collective-permute-start.4 = (f32[264,128]{1,0:T(8,128)S(1)}, f32[264,128]{1,0:T(8,128)S(1)}, u32[]{:S(2)}, u32[]{:S(2)}) collective-permute-start(f32[264,128]{1,0:T(8,128)S(1)} %pad_maximum_fusion.3), channel_id=1, source_target_pairs={{0,4},{1,5},{2,6},{3,7},{4,0},{5,1},{6,2},{7,3},{8,12},{9,13},{10,... | collective-permute-start | bytes 405512 | tf_op jit(solution)/shard_map/ppermute | solution.py:233

commit v3 on v2

v3 whole, which is shorter than its diff:
```python
import functools

import jax
import jax.numpy as jnp
from jax import lax
from jax.experimental import pallas as pl
from jax.experimental.pallas import tpu as pltpu
from jax.sharding import PartitionSpec as P

LANES = 128
SUB = 8
ROW_SIDE = 16
CHUNK = ROW_SIDE * ROW_SIDE * LANES


def log2(n):
    return n.bit_length() - 1


def parity_sign(common, bits):
    shift = 1
    while shift < bits:
        common = jnp.bitwise_xor(common, jnp.right_shift(common, shift))
        shift *= 2
    return (1 - 2 * jnp.bitwise_and(common, 1)).astype(jnp.float32)


def iota(shape, axis):
    return lax.broadcasted_iota(jnp.int32, shape, axis)


def bit_of(values, position):
    return jnp.bitwise_and(jnp.right_shift(values, position), 1)


def split(values):
    high = values.astype(jnp.bfloat16)
    low = (values - high.astype(jnp.float32)).astype(jnp.bfloat16)
    return jnp.concatenate([high, low], axis=1)


def transform_kernel(
    row_axis, order_in, amps, messages, buf, out, xs, hlane,
    order, inverse, rows_moved, lanes_moved, row_target, row_unit, lane_unit, order_sem, sems,
):
    parts, groups, length = buf.shape[0], buf.shape[1] // SUB, buf.shape[2]
    chunks = length // CHUNK
    half = CHUNK // 2
    side = ROW_SIDE * ROW_SIDE
    lane_bits, row_bits = log2(LANES), log2(ROW_SIDE)
    count = order.shape[0]

    def copies(step):
        return [
            pltpu.make_async_copy(
                amps.at[p, :, pl.ds(step * half, half)], buf.at[p, :, pl.ds(step * half, half)], sems.at[step, p]
            )
            for p in range(parts)
        ]

    order_copy = pltpu.make_async_copy(order_in, order, order_sem)
    order_copy.start()
    for step in range(2 * chunks):
        for copy in copies(step):
            copy.start()

    stacked = (2 * LANES, LANES)
    lane_sign = parity_sign(
        jnp.bitwise_and(jnp.bitwise_and(iota(stacked, 0), LANES - 1), iota(stacked, 1)), lane_bits
    )
    hlane[...] = lane_sign.astype(jnp.bfloat16)
    for p in range(count + 1):
        rows_moved[p] = lane_bits
        lanes_moved[p] = 0
    for r in range(row_bits + 1):
        lane_unit[r] = 0
    order_copy.wait()

    for j in range(count):
        inverse[order[j]] = j
    rank = jnp.int32(0)
    for p in range(lane_bits):
        lanes_moved[rank] = p
        rank = rank + (inverse[p] >= lane_bits).astype(jnp.int32)
    lane = iota((1, LANES), 1)
    lane_index = row_flip = out_row_flip = jnp.zeros((1, LANES), jnp.int32)
    rank = jnp.int32(0)
    for p in range(lane_bits, count):
        goes_to = inverse[p]
        crosses = goes_to < lane_bits
        rows_moved[rank] = p
        target = inverse[jnp.where(crosses, lanes_moved[rank], p)] - lane_bits
        row_target[p - lane_bits] = target
        row_unit[target] = 1 << p - lane_bits
        flip = jnp.left_shift(bit_of(lane, jnp.where(crosses, goes_to, 0)), target)
        out_row_flip = out_row_flip + jnp.where(crosses, flip, 0)
        rank = rank + crosses.astype(jnp.int32)
    rank = jnp.int32(0)
    for p in range(lane_bits):
        crosses = inverse[p] >= lane_bits
        partner = rows_moved[rank]
        lane_index = lane_index + jnp.left_shift(bit_of(lane, inverse[jnp.where(crosses, partner, p)]), p)
        target = row_target[jnp.where(crosses, partner - lane_bits, 0)]
        row_flip = row_flip + jnp.where(crosses, jnp.left_shift(bit_of(lane, p), target), 0)
        lane_unit[jnp.where(crosses, target, row_bits)] = 1 << p
        rank = rank + crosses.astype(jnp.int32)

    flips = [bit_of(row_flip, r) == 1 for r in range(row_bits)]
    out_flips = [bit_of(out_row_flip, r) == 1 for r in range(row_bits)]
    sources, gathers = [jnp.int32(0)], [jnp.int32(0)]
    for r in range(row_bits):
        sources = sources + [source + row_unit[r] for source in sources]
        gathers = gathers + [gather + lane_unit[r] for gather in gathers]
    gathers = [jnp.broadcast_to(jnp.bitwise_xor(lane_index, gather), (ROW_SIDE, LANES)) for gather in gathers]

    sub = iota((SUB, LANES), 0)
    masks = [bit_of(sub, level) == 0 for level in range(log2(SUB))]

    def packed_row(base, i):
        tiles = []
        for s in range(SUB):
            start = base + (s * ROW_SIDE + i) * LANES
            total = None
            for p in range(parts):
                for g in range(groups):
                    v = buf[p, g * SUB : (g + 1) * SUB, pl.ds(start, LANES)]
                    total = v * v if total is None else total + v * v
            tiles.append(total)
        for level in range(log2(SUB)):
            merged = []
            for k in range(0, len(tiles), 2):
                a, b = tiles[k] + tiles[k + 1], tiles[k] - tiles[k + 1]
                here = jnp.where(masks[level], a, b)
                other = jnp.where(masks[level], b, a)
                merged.append(here + pltpu.roll(other, SUB - (1 << level), 0))
            tiles = merged
        return tiles[0]

    def flip_rows(rows, which):
        for r in range(row_bits):
            rows = [jnp.where(which[r], rows[i ^ 1 << r], rows[i]) for i in range(ROW_SIDE)]
        return rows

    def butterfly(blocks, stride):
        return [
            blocks[c ^ stride] - blocks[c] if c & stride else blocks[c] + blocks[c ^ stride] for c in range(len(blocks))
        ]

    def arrive(step):
        for copy in copies(step):
            copy.wait()

    def sums(step, upper, total):
        base = pl.multiple_of(step * half, half)
        for i in range(ROW_SIDE):
            packed = packed_row(base, i)
            total = total + packed
            xs[i, upper * SUB : (upper + 1) * SUB, :] = packed
        return total

    def transform(c):
        rows = flip_rows([xs[source] for source in sources], flips)
        rows = [jnp.take_along_axis(rows[i], gathers[i], axis=1) for i in range(ROW_SIDE)]
        rows = flip_rows(rows, out_flips)
        for r in range(row_bits):
            rows = butterfly(rows, 1 << r)
        rows = [
            jnp.concatenate(butterfly([row[upper * SUB : (upper + 1) * SUB] for upper in range(2)], 1), axis=0)
            for row in rows
        ]
        z = jnp.dot(split(jnp.concatenate(rows, axis=0)), hlane[...], preferred_element_type=jnp.float32)
        first = pl.multiple_of(c * side, side)
        for i in range(ROW_SIDE):
            out[pl.ds(first + i, ROW_SIDE, stride=ROW_SIDE), :] = z[i * ROW_SIDE : (i + 1) * ROW_SIDE]

    def one_chunk(c, total):
        arrive(2 * c)
        transform(c - 1)
        total = sums(2 * c, 0, total)
        arrive(2 * c + 1)
        return sums(2 * c + 1, 1, total)

    total = jnp.zeros((SUB, LANES), jnp.float32)
    for upper in range(2):
        arrive(upper)
        total = sums(upper, upper, total)
    total = lax.fori_loop(1, chunks, one_chunk, total)
    transform(chunks - 1)
    total = jnp.broadcast_to(jnp.sum(total[:1], keepdims=True), (SUB, LANES))

    blocks = lax.axis_size(row_axis)
    share = out.shape[0] // blocks
    own_bit = bit_of(lax.axis_index(row_axis), 0)
    kept = messages.shape[0] // 2
    strides = [1 << k for k in range(log2(chunks))]
    apart = share // side
    rows = min(side, 4 * SUB)
    own_sign = 1.0 - 2.0 * own_bit.astype(jnp.float32)
    for start in range(0, side, rows):
        blocks_in = [out[c * side + start : c * side + start + rows, :] for c in range(chunks)]
        for stride in strides:
            if stride != apart:
                blocks_in = butterfly(blocks_in, stride)
        for c in range(chunks):
            if apart == 0:
                out[c * side + start : c * side + start + rows, :] = blocks_in[c]
            elif c & apart == 0:
                low, high = blocks_in[c], own_sign * blocks_in[c ^ apart]
                at = (c // (2 * apart) * apart + c % apart) * side + start
                messages[at : at + rows, :] = low - high
                messages[kept + at : kept + at + rows, :] = low + high
    if apart == 0:
        for at, bit in ((0, 1 - own_bit), (kept, own_bit)):
            for pair in range(blocks // 2):
                start = pl.multiple_of((2 * pair + bit) * share, share)
                messages[at + pair * share : at + (pair + 1) * share, :] = out[pl.ds(start, share), :]
    for at in (0, kept):
        messages[at + kept - SUB : at + kept, :] = total


def transform_local(amplitudes, qubit_order, row_axis):
    parts, unmeasured, length = amplitudes.shape
    chunks = length // CHUNK
    side = ROW_SIDE * ROW_SIDE
    count = qubit_order.shape[0]
    return pl.pallas_call(
        functools.partial(transform_kernel, row_axis),
        out_shape=pltpu.VMEM((chunks * side + 2 * SUB, LANES), jnp.float32),
        in_specs=[pl.BlockSpec(memory_space=pl.ANY), pl.BlockSpec(memory_space=pl.ANY)],
        out_specs=pl.BlockSpec(memory_space=pltpu.VMEM),
        scratch_shapes=[
            pltpu.VMEM((parts, unmeasured, length), jnp.float32),
            pltpu.VMEM((chunks * side, LANES), jnp.float32),
            pltpu.VMEM((ROW_SIDE, ROW_SIDE, LANES), jnp.float32),
            pltpu.VMEM((2 * LANES, LANES), jnp.bfloat16),
            pltpu.SMEM((count,), jnp.int32),
            *[pltpu.SMEM((count + 1,), jnp.int32) for _ in range(6)],
            pltpu.SemaphoreType.DMA(()),
            pltpu.SemaphoreType.DMA((2 * chunks, parts)),
        ],
        name="transform_local",
    )(qubit_order, amplitudes)


def exchange(message, axis, position):
    size = lax.axis_size(axis)
    return lax.ppermute(message, axis, [(i, i ^ 1 << position) for i in range(size)])


def local(amplitudes, qubit_order, measured_qubits):
    messages = transform_local(amplitudes, qubit_order, "row")
    rows = messages.shape[0] // 2
    joined = messages[rows:] + exchange(messages[:rows], "row", 0)
    row_bits = log2(lax.axis_size("row"))
    share = (joined.shape[0] - SUB) >> row_bits - 1
    for position in range(1, row_bits):
        pairs = joined[:-SUB].reshape(-1, 2, share, LANES)
        mass = joined[-SUB:]
        high = bit_of(lax.axis_index("row"), position) == 1
        kept = jnp.where(high, pairs[:, 1], pairs[:, 0]).reshape(-1, LANES)
        sent = jnp.where(high, pairs[:, 0], pairs[:, 1]).reshape(-1, LANES)
        joined = jnp.concatenate([kept, mass]) + exchange(jnp.concatenate([sent, mass]), "row", position)
    values, mass = joined[:-SUB], joined[-SUB:]
    for position in range(log2(lax.axis_size("col"))):
        received = exchange(jnp.concatenate([values, mass]), "col", position)
        sign = 1.0 - 2.0 * bit_of(lax.axis_index("col"), position).astype(jnp.float32)
        values = received[:-SUB] + values * sign
        mass = received[-SUB:] + mass
    total = mass[:1]
    return (values * 2.0 ** (measured_qubits / 2) / total).reshape(1, -1)


def solution(mesh):
    def program(amplitudes, qubit_order):
        measured_qubits = log2(amplitudes.shape[2])
        return jax.shard_map(
            lambda a, q: local(a, q, measured_qubits),
            mesh=mesh,
            in_specs=(P(None, "row", "col"), P()),
            out_specs=P("col", "row"),
            check_vma=False,
        )(amplitudes, qubit_order)

    return program
```

time: 33.2 us -> 31.9 us (0.961)
  Pallas kernels: 5.7 us -> 4.31 us
    pallas_call x1, Pallas kernels: 5.7 us -> 4.31 us  [transform_local(): pl.pallas_call(functools.partial(transform_kernel, row_axis), out_shape=p...]
where the time goes in v3:
time: 31.9 us; the launch traced here: 31.7 us
  waiting for transfers between devices  16.1 us (50%)
  starting transfers between devices  10.4 us (33%)
  Pallas kernels  4.31 us (14%)
  other arithmetic  0.84 us (3%)
    ppermute x5, waiting for transfers between devices, exchange(): lax.ppermute(message, axis, [(i, i ^ 1 << position) for i in range(size)])  16.1 us
    ppermute x5, starting transfers between devices, exchange(): lax.ppermute(message, axis, [(i, i ^ 1 << position) for i in range(size)])  10.4 us
    pallas_call x1, Pallas kernels, transform_local(): pl.pallas_call(functools.partial(transform_kernel, row_axis), out_shape=p...  4.31 us
    div x1, other arithmetic, local(): return (values * 2.0 ** (measured_qubits / 2) / total).reshape(1, -1)  0.68 us
  transfers between devices with their start and end apart: 5, of which 5 were waited for; matrix products, arithmetic and copies ran while one was open for 0% of the time, Pallas kernels for 0%

profile of v3, /device:TPU:0, one launch (start us, length us, event | category | flops | bytes accessed | tf_op | source)
XLA Modules:
  0.0 31.7 jit_solution(8261204878872090415)
XLA Ops:
  0.0 4.3 %transform_local.1 = f32[1040,128]{1,0:T(8,128)S(1)} custom-call(s32[11]{0:T(128)} %order_in.1, f32[2,8,131072]{2,1,0:T(8,128)} %amps.1), custom_call_target="tpu_custom_call" | custom-call | tf_op jit(solution)/shard_map/transform_local/pallas_call | solution.py:226
  4.3 0.6 %collective-permute-start = (f32[520,128]{1,0:T(8,128)S(1)}, f32[520,128]{1,0:T(8,128)S(1)}, u32[]{:S(2)}, u32[]{:S(2)}) collective-permute-start(f32[520,128]{1,0:T(8,128)S(1)} %slice.64), channel_id=1, source_target_pairs={{0,8},{8,0},{16,24},{24,16},{1,9},{9,1},{17,25},{25,17},{2,10},{10... | collective-permute-start | bytes 798728 | tf_op jit(solution)/shard_map/ppermute | solution.py:247
  4.9 1.2 %collective-permute-done = f32[520,128]{1,0:T(8,128)S(1)} collective-permute-done((f32[520,128]{1,0:T(8,128)S(1)}, f32[520,128]{1,0:T(8,128)S(1)}, u32[]{:S(2)}, u32[]{:S(2)}) %collective-permute-start) | collective-permute-done | bytes 266272 | tf_op jit(solution)/shard_map/ppermute | solution.py:247
  6.2 2.9 %collective-permute-start.1 = (f32[264,128]{1,0:T(8,128)S(1)}, f32[264,128]{1,0:T(8,128)S(1)}, u32[]{:S(2)}, u32[]{:S(2)}) collective-permute-start(f32[264,128]{1,0:T(8,128)S(1)} %pad_maximum_fusion), channel_id=1, source_target_pairs={{0,16},{8,24},{16,0},{24,8},{1,17},{9,25},{17,1},{25,9},{2,18},{10... | collective-permute-start | bytes 405512 | tf_op jit(solution)/shard_map/ppermute | solution.py:247
  9.2 3.9 %collective-permute-done.1 = f32[264,128]{1,0:T(8,128)S(1)} collective-permute-done((f32[264,128]{1,0:T(8,128)S(1)}, f32[264,128]{1,0:T(8,128)S(1)}, u32[]{:S(2)}, u32[]{:S(2)}) %collective-permute-start.1) | collective-permute-done | bytes 135200 | tf_op jit(solution)/shard_map/ppermute | solution.py:247
  13.1 1.8 %collective-permute-start.2 = (f32[264,128]{1,0:T(8,128)S(1)}, f32[264,128]{1,0:T(8,128)S(1)}, u32[]{:S(2)}, u32[]{:S(2)}) collective-permute-start(f32[264,128]{1,0:T(8,128)S(1)} %fusion), channel_id=1, source_target_pairs={{0,1},{1,0},{2,3},{3,2},{4,5},{5,4},{6,7},{7,6},{8,9},{9,8},{10,11... | collective-permute-start | bytes 405512 | tf_op jit(solution)/shard_map/ppermute | solution.py:247
  14.8 3.3 %collective-permute-done.2 = f32[264,128]{1,0:T(8,128)S(1)} collective-permute-done((f32[264,128]{1,0:T(8,128)S(1)}, f32[264,128]{1,0:T(8,128)S(1)}, u32[]{:S(2)}, u32[]{:S(2)}) %collective-permute-start.2) | collective-permute-done | bytes 135200 | tf_op jit(solution)/shard_map/ppermute | solution.py:247
  18.2 1.8 %collective-permute-start.3 = (f32[264,128]{1,0:T(8,128)S(1)}, f32[264,128]{1,0:T(8,128)S(1)}, u32[]{:S(2)}, u32[]{:S(2)}) collective-permute-start(f32[264,128]{1,0:T(8,128)S(1)} %pad_maximum_fusion.2), channel_id=1, source_target_pairs={{0,2},{1,3},{2,0},{3,1},{4,6},{5,7},{6,4},{7,5},{8,10},{9,11},{10,... | collective-permute-start | bytes 405512 | tf_op jit(solution)/shard_map/ppermute | solution.py:247
  20.0 3.3 %collective-permute-done.3 = f32[264,128]{1,0:T(8,128)S(1)} collective-permute-done((f32[264,128]{1,0:T(8,128)S(1)}, f32[264,128]{1,0:T(8,128)S(1)}, u32[]{:S(2)}, u32[]{:S(2)}) %collective-permute-start.3) | collective-permute-done | bytes 135200 | tf_op jit(solution)/shard_map/ppermute | solution.py:247
  23.3 3.3 %collective-permute-start.4 = (f32[264,128]{1,0:T(8,128)S(1)}, f32[264,128]{1,0:T(8,128)S(1)}, u32[]{:S(2)}, u32[]{:S(2)}) collective-permute-start(f32[264,128]{1,0:T(8,128)S(1)} %pad_maximum_fusion.3), channel_id=1, source_target_pairs={{0,4},{1,5},{2,6},{3,7},{4,0},{5,1},{6,2},{7,3},{8,12},{9,13},{10,... | collective-permute-start | bytes 405512 | tf_op jit(solution)/shard_map/ppermute | solution.py:247
  26.6 4.4 %collective-permute-done.4 = f32[264,128]{1,0:T(8,128)S(1)} collective-permute-done((f32[264,128]{1,0:T(8,128)S(1)}, f32[264,128]{1,0:T(8,128)S(1)}, u32[]{:S(2)}, u32[]{:S(2)}) %collective-permute-start.4) | collective-permute-done | bytes 135200 | tf_op jit(solution)/shard_map/ppermute | solution.py:247
  31.0 0.7 %fusion.2 = f32[256,128]{1,0:T(8,128)} fusion(f32[264,128]{1,0:T(8,128)S(1)} %collective-permute-done.4, f32[256,128]{1,0:T(8,128)S(1)} %slice_add_fusion.2, f32[128]{0:T(128)S(1)} %slice_bitcast_fusion, f32[]{:T(128)S(6)} %sub.11), kind=kLoop, calls=%fused_computation.8 | loop fusion | flops 131072 | bytes 393732 | tf_op jit(solution)/shard_map/div | solution.py:270
  (15 shorter events, 0.2 us)
Async XLA Ops:
  4.3 1.7 %collective-permute-start = (f32[520,128]{1,0:T(8,128)S(1)}, f32[520,128]{1,0:T(8,128)S(1)}, u32[]{:S(2)}, u32[]{:S(2)}) collective-permute-start(f32[520,128]{1,0:T(8,128)S(1)} %slice.64), channel_id=1, source_target_pairs={{0,8},{8,0},{16,24},{24,16},{1,9},{9,1},{17,25},{25,17},{2,10},{10... | collective-permute-start | bytes 798728 | tf_op jit(solution)/shard_map/ppermute | solution.py:247
  6.2 6.8 %collective-permute-start.1 = (f32[264,128]{1,0:T(8,128)S(1)}, f32[264,128]{1,0:T(8,128)S(1)}, u32[]{:S(2)}, u32[]{:S(2)}) collective-permute-start(f32[264,128]{1,0:T(8,128)S(1)} %pad_maximum_fusion), channel_id=1, source_target_pairs={{0,16},{8,24},{16,0},{24,8},{1,17},{9,25},{17,1},{25,9},{2,18},{10... | collective-permute-start | bytes 405512 | tf_op jit(solution)/shard_map/ppermute | solution.py:247
  13.1 5.1 %collective-permute-start.2 = (f32[264,128]{1,0:T(8,128)S(1)}, f32[264,128]{1,0:T(8,128)S(1)}, u32[]{:S(2)}, u32[]{:S(2)}) collective-permute-start(f32[264,128]{1,0:T(8,128)S(1)} %fusion), channel_id=1, source_target_pairs={{0,1},{1,0},{2,3},{3,2},{4,5},{5,4},{6,7},{7,6},{8,9},{9,8},{10,11... | collective-permute-start | bytes 405512 | tf_op jit(solution)/shard_map/ppermute | solution.py:247
  18.2 5.1 %collective-permute-start.3 = (f32[264,128]{1,0:T(8,128)S(1)}, f32[264,128]{1,0:T(8,128)S(1)}, u32[]{:S(2)}, u32[]{:S(2)}) collective-permute-start(f32[264,128]{1,0:T(8,128)S(1)} %pad_maximum_fusion.2), channel_id=1, source_target_pairs={{0,2},{1,3},{2,0},{3,1},{4,6},{5,7},{6,4},{7,5},{8,10},{9,11},{10,... | collective-permute-start | bytes 405512 | tf_op jit(solution)/shard_map/ppermute | solution.py:247
  23.3 7.7 %collective-permute-start.4 = (f32[264,128]{1,0:T(8,128)S(1)}, f32[264,128]{1,0:T(8,128)S(1)}, u32[]{:S(2)}, u32[]{:S(2)}) collective-permute-start(f32[264,128]{1,0:T(8,128)S(1)} %pad_maximum_fusion.3), channel_id=1, source_target_pairs={{0,4},{1,5},{2,6},{3,7},{4,0},{5,1},{6,2},{7,3},{8,12},{9,13},{10,... | collective-permute-start | bytes 405512 | tf_op jit(solution)/shard_map/ppermute | solution.py:247
